TPU v7x, 32 devices: a whole 2x2x4 slice. The times are simulated.
32 devices in a mesh: vocab: 8 (over y, x, core), seq: 4 (over z).
Axes of the slice: x: 2, y: 2, z: 4, core: 2. Of those that a mesh axis runs over, the one named last changes fastest.
Arguments:
- latent_vector: bfloat16 [32, 7168], P('vocab', 'seq'), may hold values from -400 to 400
- unembedding_matrix: bfloat16 [7168, 8192], P('seq', 'vocab'), may hold values from -0.0625 to 0.0625
- occurrence_tally: int32 [32, 8192], P(('seq', 'vocab')), may hold values from 0 to 2
- additive_offset_table: bfloat16 [32, 8192], P(('seq', 'vocab')), may hold values from 0 to 0.5
- recurrence_charge: float32 [32], P(('seq', 'vocab')), may hold values from 0.05 to 0.5
- appearance_charge: float32 [32], P(('seq', 'vocab')), may hold values from 0.6 to 1.5
- recurrence_divisor: float32 [32], P('seq'), may hold values from 1.05 to 1.6
- softening_divisor: float32 [32], P('seq'), may hold values from 0.5 to 1.5
- nucleus_share_limit: float32 [32], P('seq'), may hold values from 0.5 to 0.95
Outputs:
- penalized_logits: bfloat16 [32, 8192], P('seq', 'vocab')
- cutoff: float32 [32], P('seq')
Inputs may be any that keep to these rules, and one draw needn't show every extreme that they name: `appearance_charge`: each sequence's presence penalty exceeds every entry of its token bias.
All inputs are finite; a program needn't handle non-finite values.
Results may differ from a plain program's by a relative error of at most 0.0047.
Values may be sent and summed in bfloat16 or wider, within the bound.
No kernel may reach another device: no remote copies, remote signals or barrier semaphores. Data moves between devices by JAX's collectives and lax.ppermute only.
A program may use at most 64 MiB of HBM per device.

v0:
```python
import jax
import jax.numpy as jnp
from jax import lax
from jax.sharding import PartitionSpec as P

STEPS = 9
cutoff_span = 32.0


def per_device(
    latent_vector,
    unembedding_matrix,
    occurrence_tally,
    additive_offset_table,
    recurrence_charge,
    appearance_charge,
    recurrence_divisor,
    softening_divisor,
    nucleus_share_limit,
):
    count_float = occurrence_tally.astype(jnp.float32)
    offset = (
        additive_offset_table.astype(jnp.float32)
        - recurrence_charge[:, None] * count_float
        - appearance_charge[:, None] * (occurrence_tally > 0).astype(jnp.float32)
    ).astype(jnp.bfloat16)
    relaid = lax.all_to_all(offset, "vocab", split_axis=1, concat_axis=0, tiled=True)
    partial_logits = jnp.dot(
        lax.all_gather(latent_vector, "vocab", axis=0, tiled=True),
        unembedding_matrix,
        preferred_element_type=jnp.float32,
    )
    logits = lax.psum_scatter(partial_logits, "seq", scatter_dimension=0, tiled=True)
    seen_mask = relaid < 0
    factor = recurrence_divisor[:, None]
    discouraged_scores = jnp.where(
        seen_mask, jnp.where(logits > 0, logits / factor, logits * factor), logits
    ) + relaid.astype(jnp.float32)
    softened_scores = discouraged_scores / softening_divisor[:, None]
    largest_score = lax.pmax(jnp.max(softened_scores, axis=1), "vocab")
    exponential_values = jnp.exp(softened_scores - largest_score[:, None])
    row_total = lax.psum(jnp.sum(exponential_values, axis=1), "vocab")
    target = nucleus_share_limit * row_total
    start_bounds = (jnp.zeros_like(largest_score), jnp.ones_like(largest_score))
    fractions = jnp.arange(1, 8, dtype=jnp.float32)

    def refine(turn_index, bounds):
        lower_end, upper_end = bounds
        stride = (upper_end - lower_end) * 0.125
        probes = lower_end[:, None] + stride[:, None] * fractions[None, :]
        threshold_candidates = largest_score[:, None] - cutoff_span * probes
        inside = softened_scores[:, None, :] >= threshold_candidates[:, :, None]
        partial_mass = jnp.sum(jnp.where(inside, exponential_values[:, None, :], 0.0), axis=2)
        cumulative_shares = lax.psum(partial_mass, "vocab")
        below_count = jnp.sum((cumulative_shares < target[:, None]).astype(jnp.float32), axis=1)
        new_lower = lower_end + stride * below_count
        return (new_lower, new_lower + stride)

    lower_end, upper_end = lax.fori_loop(0, STEPS // 3, refine, start_bounds)
    return (discouraged_scores.astype(jnp.bfloat16), largest_score - cutoff_span * upper_end)


def solution(mesh):
    in_specs = (
        P("vocab", "seq"),
        P("seq", "vocab"),
        P(("seq", "vocab"), None),
        P(("seq", "vocab"), None),
        P(("seq", "vocab")),
        P(("seq", "vocab")),
        P("seq"),
        P("seq"),
        P("seq"),
    )
    out_specs = (P("seq", "vocab"), P("seq"))
    return jax.shard_map(
        per_device, mesh=mesh, in_specs=in_specs, out_specs=out_specs, check_vma=False
    )
```

profile of v0, /device:TPU:0, one launch (start us, length us, event | category | flops | bytes accessed | tf_op | source)
XLA Modules:
  0.0 110.7 jit_solution(10906374789269794412)
XLA Ops:
  7.2 0.0 copy-start
  7.2 0.0 copy-start.1
  7.2 0.0 copy-start.3
  7.2 0.0 copy-start.2
  7.2 0.0 copy-start.4
  7.2 0.0 reduce-scatter.2.cloned.1.call-start
  7.3 10.9 %all-gather = bf16[8,4,1792]{2,1,0:T(4,128)(2,1)S(1)} all-gather(bf16[1,4,1792]{2,1,0:T(4,128)(2,1)} %bitcast.19), channel_id=1, replica_groups=mesh['vocab'=8,'seq'=4] {'vocab'}, dimensions={0}, use_global_device_ids=true | all-gather | bytes 129024 | tf_op jit(solution)/shard_map/all_gather | solution.py:29
  18.2 3.4 %fusion.9 = f32[32,1024]{1,0:T(8,128)} fusion(bf16[32,1792]{1,0:T(8,128)(2,1)S(1)} %reshape.88, bf16[1792,1024]{1,0:T(8,128)(2,1)} %param.12), kind=kOutput, calls=%fused_computation.20 | convolution fusion | flops 117440512 | bytes 3915776 | tf_op jit(solution)/shard_map/dot_general | solution.py:28
  21.6 0.0 reduce-scatter.2.cloned.1.call-update
  22.9 0.0 copy-done
  23.0 0.0 copy-done.1
  23.0 0.1 fusion.5
  23.0 0.5 broadcast.112
  23.6 0.7 reduce
  24.3 0.6 reshape.89
  24.9 3.3 %all-to-all-start = ((bf16[8,2,512]{2,1,0:T(2,128)(2,1)}), bf16[8,2,512]{2,1,0:T(2,128)(2,1)S(1)}, u32[]{:S(2)}, u32[]{:S(2)}) async-start(bf16[8,2,512]{2,1,0:T(2,128)(2,1)} %reshape.89), calls=%async_computation | async-start | bytes 32768 | tf_op jit(solution)/shard_map/all_to_all | solution.py:27
  28.3 4.7 %all-to-all-done = bf16[8,2,512]{2,1,0:T(2,128)(2,1)S(1)} async-done(((bf16[8,2,512]{2,1,0:T(2,128)(2,1)}), bf16[8,2,512]{2,1,0:T(2,128)(2,1)S(1)}, u32[]{:S(2)}, u32[]{:S(2)}) %all-to-all-start) | async-done | bytes 16416 | tf_op jit(solution)/shard_map/all_to_all | solution.py:27
  33.0 8.5 %reduce-scatter.2.cloned.1.call-done = f32[8,1024]{1,0:T(8,128)} async-done(((f32[32,1024]{1,0:T(8,128)}), f32[8,1024]{1,0:T(8,128)}) %reduce-scatter.2.cloned.1.call-update) | async-done | bytes 32784 | tf_op jit(solution)/shard_map/reduce_scatter | solution.py:33
  41.5 0.0 copy-done.3
  41.5 0.0 copy-done.2
  41.5 1.6 %fusion.8 = (f32[8]{0:T(128)S(1)}, f32[8,1024]{1,0:T(8,128)S(1)}, bf16[8,1024]{1,0:T(8,128)(2,1)}) fusion(f32[8]{0:T(128)S(1)} %copy-done.2, f32[8,1024]{1,0:T(8,128)} %reduce-scatter.2.cloned.1.call-done, f32[8]{0:T(128)S(1)} %copy-done.3, bf16[1,8,1024]{2,0,1:T(2,128)(2,1)S(1)} %bitcast.17), kind=kLoop, calls=%fused_computation.19 | loop fusion | flops 90104 | bytes 98400 | tf_op jit(solution)/shard_map/reduce_max | solution.py:40
  43.1 11.8 %pmax.7 = f32[8]{0:T(128)S(1)} all-reduce(f32[8]{0:T(128)S(1)} %get-tuple-element.91), channel_id=1, replica_groups=mesh['vocab'=8,'seq'=4] {'vocab'}, use_global_device_ids=true, to_apply=%region_2.3 | all-reduce | flops 8 | bytes 64 | tf_op jit(solution)/shard_map/pmax | solution.py:40
  54.9 0.2 fusion.7
  55.1 11.9 %psum.14 = f32[8]{0:T(128)S(1)} all-reduce(f32[8]{0:T(128)S(1)} %get-tuple-element.89), channel_id=1, replica_groups=mesh['vocab'=8,'seq'=4] {'vocab'}, use_global_device_ids=true, to_apply=%region_4.5 | all-reduce | flops 8 | bytes 64 | tf_op jit(solution)/shard_map/psum | solution.py:42
  66.9 0.0 copy-done.4
  66.9 36.4 %while.13 = (s32[]{:T(128)}, f32[8]{0:T(128)S(1)}, f32[8]{0:T(128)S(1)}, f32[8,1024]{1,0:T(8,128)S(1)}, f32[8]{0:T(128)S(1)}, /*index=5*/f32[8,1024]{1,0:T(8,128)S(1)}, f32[8]{0:T(128)S(1)}, s32[]{:T(128)}, s32[]{:T(128)}) while((s32[]{:T(128)}, f32[8]{0:T(128)S(1)}, f32[8]{0:T(128)S(1)}, f32[8,1024]{1,0:T(8,128)S(1)}, ...), condition=%wide.region_9.10_spmd.clone, body=%wide.region_5.9_spmd.clone.sunk | while | flops 172482 | bytes 67487 | solution.py:59
  67.0 0.1 multiply_subtract_fusion.3
  67.0 0.2 select_reduce_fusion.2
  67.2 11.8 %psum.17 = f32[8,7]{0,1:T(8,128)S(1)} all-reduce(f32[8,7]{0,1:T(8,128)S(1)} %select_reduce_fusion.2), channel_id=1, replica_groups=mesh['vocab'=8,'seq'=4] {'vocab'}, use_global_device_ids=true, to_apply=%region_7.7 | all-reduce | flops 56 | bytes 448 | tf_op jit(solution)/shard_map/while/body/eval_jaxpr/psum | solution.py:54
  79.1 0.1 multiply_subtract_fusion.3
  79.2 0.2 select_reduce_fusion.2
  79.3 11.8 %psum.17 = f32[8,7]{0,1:T(8,128)S(1)} all-reduce(f32[8,7]{0,1:T(8,128)S(1)} %select_reduce_fusion.2), channel_id=1, replica_groups=mesh['vocab'=8,'seq'=4] {'vocab'}, use_global_device_ids=true, to_apply=%region_7.7 | all-reduce | flops 56 | bytes 448 | tf_op jit(solution)/shard_map/while/body/eval_jaxpr/psum | solution.py:54
  91.2 0.1 multiply_subtract_fusion.3
  91.3 0.2 select_reduce_fusion.2
  91.5 11.8 %psum.17 = f32[8,7]{0,1:T(8,128)S(1)} all-reduce(f32[8,7]{0,1:T(8,128)S(1)} %select_reduce_fusion.2), channel_id=1, replica_groups=mesh['vocab'=8,'seq'=4] {'vocab'}, use_global_device_ids=true, to_apply=%region_7.7 | all-reduce | flops 56 | bytes 448 | tf_op jit(solution)/shard_map/while/body/eval_jaxpr/psum | solution.py:54
  103.3 0.5 multiply_subtract_fusion.1
  (17 shorter events, 0.2 us)
Async XLA Ops:
  7.2 15.8 %copy-start = (s32[1,8192]{1,0:T(1,128)S(1)}, s32[1,8192]{1,0:T(1,128)}, u32[]{:S(2)}) copy-start(s32[1,8192]{1,0:T(1,128)} %param.13) | copy-start | bytes 98308
  7.2 15.8 %copy-start.1 = (bf16[1,8192]{1,0:T(2,128)(2,1)S(1)}, bf16[1,8192]{1,0:T(2,128)(2,1)}, u32[]{:S(2)}) copy-start(bf16[1,8192]{1,0:T(2,128)(2,1)} %param.14) | copy-start | bytes 49156
  7.2 34.3 %copy-start.3 = (f32[8]{0:T(128)S(1)}, f32[8]{0:T(128)}, u32[]{:S(2)}) copy-start(f32[8]{0:T(128)} %param.17) | copy-start | bytes 100
  7.2 34.3 %copy-start.2 = (f32[8]{0:T(128)S(1)}, f32[8]{0:T(128)}, u32[]{:S(2)}) copy-start(f32[8]{0:T(128)} %param.18) | copy-start | bytes 100
  7.2 59.7 %copy-start.4 = (f32[8]{0:T(128)S(1)}, f32[8]{0:T(128)}, u32[]{:S(2)}) copy-start(f32[8]{0:T(128)} %param.19) | copy-start | bytes 100
  7.2 34.3 %reduce-scatter.2.cloned.1.call-start = ((), (), s32[]{:S(2)}) async-start(), calls=%async_computation.2 | async-start | bytes 163840 | tf_op jit(solution)/shard_map/reduce_scatter | solution.py:33
  24.9 8.0 %all-to-all-start = ((bf16[8,2,512]{2,1,0:T(2,128)(2,1)}), bf16[8,2,512]{2,1,0:T(2,128)(2,1)S(1)}, u32[]{:S(2)}, u32[]{:S(2)}) async-start(bf16[8,2,512]{2,1,0:T(2,128)(2,1)} %reshape.89), calls=%async_computation | async-start | bytes 32768 | tf_op jit(solution)/shard_map/all_to_all | solution.py:27
Sparse Core Ops, SparseCore 0:
  21.8 19.6 reduce-scatter.1
where the time goes:
time: 111 us
  blocking collectives  70 us (63%)
  between operations  15.4 us (14%)
  waiting for transfers between devices  13.2 us (12%)
  other arithmetic  3.96 us (4%)
  matrix products  3.42 us (3%)
  starting transfers between devices  3.37 us (3%)
  local copies, waits for them, and re-layouts  1.2 us (1%)
    psum x3, blocking collectives, refine(): cumulative_shares = lax.psum(partial_mass, 'vocab')  35.4 us
    psum x1, blocking collectives, per_device(): row_total = lax.psum(jnp.sum(exponential_values, axis=1), 'vocab')  11.9 us
    pmax x1, blocking collectives, per_device(): largest_score = lax.pmax(jnp.max(softened_scores, axis=1), 'vocab')  11.8 us
    all_gather x1, blocking collectives, per_device(): lax.all_gather(latent_vector, 'vocab', axis=0, tiled=True)  10.9 us
    reduce_scatter x1, waiting for transfers between devices, per_device(): lax.psum_scatter(partial_logits, 'seq', scatter_dimension=0, tiled=True)  8.54 us
    all_to_all x1, waiting for transfers between devices, per_device(): lax.all_to_all(offset, 'vocab', split_axis=1, concat_axis=0, tiled=True)  4.67 us
    dot_general x1, matrix products, per_device(): jnp.dot(lax.all_gather(latent_vector, 'vocab', axis=0, tiled=True), unemb...  3.42 us
    all_to_all x1, starting transfers between devices, per_device(): lax.all_to_all(offset, 'vocab', split_axis=1, concat_axis=0, tiled=True)  3.34 us
  transfers between devices with their start and end apart: 2, of which 2 were waited for; matrix products, arithmetic and copies ran while one was open for 2% of the time, Pallas kernels for 0%

commit v1 on v0

--- a/solution.py
+++ b/solution.py
@@ -51,7 +51,11 @@
         threshold_candidates = largest_score[:, None] - cutoff_span * probes
         inside = softened_scores[:, None, :] >= threshold_candidates[:, :, None]
         partial_mass = jnp.sum(jnp.where(inside, exponential_values[:, None, :], 0.0), axis=2)
-        cumulative_shares = lax.psum(partial_mass, "vocab")
+        cumulative_shares = partial_mass
+        for hop in (1, 2, 4):
+            cumulative_shares = cumulative_shares + lax.ppermute(
+                cumulative_shares, "vocab", [(dev, dev ^ hop) for dev in range(8)]
+            )
         below_count = jnp.sum((cumulative_shares < target[:, None]).astype(jnp.float32), axis=1)
         new_lower = lower_end + stride * below_count
         return (new_lower, new_lower + stride)

time: 111 us -> 101 us (0.910)
  blocking collectives: 70 us -> 34.6 us
  waiting for transfers between devices: 13.2 us -> 34 us
  starting transfers between devices: 3.37 us -> 7.87 us
    psum x3 -> x0, blocking collectives: 35.4 us -> none  [refine(): cumulative_shares = lax.psum(partial_mass, 'vocab')]
    ppermute x0 -> x9, waiting for transfers between devices: none -> 20.8 us  [refine(): lax.ppermute(cumulative_shares, 'vocab', [(dev, dev ^ hop) for dev in ran...]
    ppermute x0 -> x9, starting transfers between devices: none -> 4.5 us  [refine(): lax.ppermute(cumulative_shares, 'vocab', [(dev, dev ^ hop) for dev in ran...]
  transfers between devices with their start and end apart: 2 -> 11, of which waited for: 2 -> 11; matrix products, arithmetic and copies ran while one was open for 2% -> 2% of each run, Pallas kernels for 0% -> 0%
where the time goes in v1:
time: 101 us
  blocking collectives  34.6 us (34%)
  waiting for transfers between devices  34 us (34%)
  between operations  15.4 us (15%)
  starting transfers between devices  7.87 us (8%)
  other arithmetic  3.98 us (4%)
  matrix products  3.42 us (3%)
  local copies, waits for them, and re-layouts  1.2 us (1%)
    ppermute x9, waiting for transfers between devices, refine(): lax.ppermute(cumulative_shares, 'vocab', [(dev, dev ^ hop) for dev in ran...  20.8 us
    psum x1, blocking collectives, per_device(): row_total = lax.psum(jnp.sum(exponential_values, axis=1), 'vocab')  11.9 us
    pmax x1, blocking collectives, per_device(): largest_score = lax.pmax(jnp.max(softened_scores, axis=1), 'vocab')  11.8 us
    all_gather x1, blocking collectives, per_device(): lax.all_gather(latent_vector, 'vocab', axis=0, tiled=True)  10.9 us
    reduce_scatter x1, waiting for transfers between devices, per_device(): lax.psum_scatter(partial_logits, 'seq', scatter_dimension=0, tiled=True)  8.54 us
    all_to_all x1, waiting for transfers between devices, per_device(): lax.all_to_all(offset, 'vocab', split_axis=1, concat_axis=0, tiled=True)  4.67 us
    ppermute x9, starting transfers between devices, refine(): lax.ppermute(cumulative_shares, 'vocab', [(dev, dev ^ hop) for dev in ran...  4.5 us
    dot_general x1, matrix products, per_device(): jnp.dot(lax.all_gather(latent_vector, 'vocab', axis=0, tiled=True), unemb...  3.42 us
  transfers between devices with their start and end apart: 11, of which 11 were waited for; matrix products, arithmetic and copies ran while one was open for 2% of the time, Pallas kernels for 0%

profile of v1, /device:TPU:0, one launch (start us, length us, event | category | flops | bytes accessed | tf_op | source)
XLA Modules:
  0.0 100.6 jit_solution(15620220102057839805)
XLA Ops:
  7.2 0.0 copy-start
  7.2 0.0 copy-start.1
  7.2 0.0 copy-start.3
  7.2 0.0 copy-start.2
  7.2 0.0 copy-start.4
  7.2 0.0 reduce-scatter.2.cloned.1.call-start
  7.3 10.9 %all-gather = bf16[8,4,1792]{2,1,0:T(4,128)(2,1)S(1)} all-gather(bf16[1,4,1792]{2,1,0:T(4,128)(2,1)} %bitcast.19), channel_id=1, replica_groups=mesh['vocab'=8,'seq'=4] {'vocab'}, dimensions={0}, use_global_device_ids=true | all-gather | bytes 129024 | tf_op jit(solution)/shard_map/all_gather | solution.py:29
  18.2 3.4 %fusion.9 = f32[32,1024]{1,0:T(8,128)} fusion(bf16[32,1792]{1,0:T(8,128)(2,1)S(1)} %reshape.88, bf16[1792,1024]{1,0:T(8,128)(2,1)} %param.12), kind=kOutput, calls=%fused_computation.21 | convolution fusion | flops 117440512 | bytes 3915776 | tf_op jit(solution)/shard_map/dot_general | solution.py:28
  21.6 0.0 reduce-scatter.2.cloned.1.call-update
  22.9 0.0 copy-done
  23.0 0.1 fusion.5
  23.0 0.5 broadcast.112
  23.6 0.7 reduce
  24.3 0.6 reshape.89
  24.9 3.3 %all-to-all-start = ((bf16[8,2,512]{2,1,0:T(2,128)(2,1)}), bf16[8,2,512]{2,1,0:T(2,128)(2,1)S(1)}, u32[]{:S(2)}, u32[]{:S(2)}) async-start(bf16[8,2,512]{2,1,0:T(2,128)(2,1)} %reshape.89), calls=%async_computation | async-start | bytes 32768 | tf_op jit(solution)/shard_map/all_to_all | solution.py:27
  28.3 4.7 %all-to-all-done = bf16[8,2,512]{2,1,0:T(2,128)(2,1)S(1)} async-done(((bf16[8,2,512]{2,1,0:T(2,128)(2,1)}), bf16[8,2,512]{2,1,0:T(2,128)(2,1)S(1)}, u32[]{:S(2)}, u32[]{:S(2)}) %all-to-all-start) | async-done | bytes 16416 | tf_op jit(solution)/shard_map/all_to_all | solution.py:27
  33.0 8.5 %reduce-scatter.2.cloned.1.call-done = f32[8,1024]{1,0:T(8,128)} async-done(((f32[32,1024]{1,0:T(8,128)}), f32[8,1024]{1,0:T(8,128)}) %reduce-scatter.2.cloned.1.call-update) | async-done | bytes 32784 | tf_op jit(solution)/shard_map/reduce_scatter | solution.py:33
  41.5 0.0 copy-done.3
  41.5 1.6 %fusion.8 = (f32[8]{0:T(128)S(1)}, f32[8,1024]{1,0:T(8,128)S(1)}, bf16[8,1024]{1,0:T(8,128)(2,1)}) fusion(f32[8]{0:T(128)S(1)} %copy-done.2, f32[8,1024]{1,0:T(8,128)} %reduce-scatter.2.cloned.1.call-done, f32[8]{0:T(128)S(1)} %copy-done.3, bf16[1,8,1024]{2,0,1:T(2,128)(2,1)S(1)} %bitcast.17), kind=kLoop, calls=%fused_computation.20 | loop fusion | flops 90104 | bytes 98400 | tf_op jit(solution)/shard_map/reduce_max | solution.py:40
  43.1 11.8 %pmax.7 = f32[8]{0:T(128)S(1)} all-reduce(f32[8]{0:T(128)S(1)} %get-tuple-element.91), channel_id=1, replica_groups=mesh['vocab'=8,'seq'=4] {'vocab'}, use_global_device_ids=true, to_apply=%region_2.3 | all-reduce | flops 8 | bytes 64 | tf_op jit(solution)/shard_map/pmax | solution.py:40
  54.9 0.2 fusion.7
  55.1 11.9 %psum.7 = f32[8]{0:T(128)S(1)} all-reduce(f32[8]{0:T(128)S(1)} %get-tuple-element.89), channel_id=1, replica_groups=mesh['vocab'=8,'seq'=4] {'vocab'}, use_global_device_ids=true, to_apply=%region_4.5 | all-reduce | flops 8 | bytes 64 | tf_op jit(solution)/shard_map/psum | solution.py:42
  66.9 26.3 %while.13 = (s32[]{:T(128)}, f32[8]{0:T(128)S(1)}, f32[8]{0:T(128)S(1)}, f32[8,1024]{1,0:T(8,128)S(1)}, f32[8]{0:T(128)S(1)}, /*index=5*/f32[8,1024]{1,0:T(8,128)S(1)}, f32[8]{0:T(128)S(1)}, s32[]{:T(128)}, s32[]{:T(128)}) while((s32[]{:T(128)}, f32[8]{0:T(128)S(1)}, f32[8]{0:T(128)S(1)}, f32[8,1024]{1,0:T(8,128)S(1)}, ...), condition=%wide.region_8.9_spmd.clone, body=%wide.region_5.8_spmd.clone.sunk | while | flops 172594 | bytes 71415 | solution.py:63
  67.0 0.1 multiply_subtract_fusion.3
  67.1 0.2 select_reduce_fusion.2
  67.2 0.1 collective-permute-start
  67.3 1.2 %collective-permute-done = f32[8,7]{0,1:T(8,128)S(1)} collective-permute-done((f32[8,7]{0,1:T(8,128)S(1)}, f32[8,7]{0,1:T(8,128)S(1)}, u32[]{:S(2)}, u32[]{:S(2)}) %collective-permute-start) | collective-permute-done | bytes 256 | tf_op jit(solution)/shard_map/while/body/eval_jaxpr/ppermute | solution.py:56
  68.5 0.0 collective-permute-start.1
  68.5 3.6 %collective-permute-done.1 = f32[8,7]{0,1:T(8,128)S(1)} collective-permute-done((f32[8,7]{0,1:T(8,128)S(1)}, f32[8,7]{0,1:T(8,128)S(1)}, u32[]{:S(2)}, u32[]{:S(2)}) %collective-permute-start.1) | collective-permute-done | bytes 256 | tf_op jit(solution)/shard_map/while/body/eval_jaxpr/ppermute | solution.py:56
  72.1 1.4 %collective-permute-start.2 = (f32[8,7]{0,1:T(8,128)S(1)}, f32[8,7]{0,1:T(8,128)S(1)}, u32[]{:S(2)}, u32[]{:S(2)}) collective-permute-start(f32[8,7]{0,1:T(8,128)S(1)} %add.81), channel_id=1, source_target_pairs={{0,16},{4,20},{8,24},{12,28},{16,0},{20,4},{24,8},{28,12},{1,17},{... | collective-permute-start | bytes 680 | tf_op jit(solution)/shard_map/while/body/eval_jaxpr/ppermute | solution.py:56
  73.5 2.2 %collective-permute-done.2 = f32[8,7]{0,1:T(8,128)S(1)} collective-permute-done((f32[8,7]{0,1:T(8,128)S(1)}, f32[8,7]{0,1:T(8,128)S(1)}, u32[]{:S(2)}, u32[]{:S(2)}) %collective-permute-start.2) | collective-permute-done | bytes 256 | tf_op jit(solution)/shard_map/while/body/eval_jaxpr/ppermute | solution.py:56
  75.8 0.1 multiply_subtract_fusion.3
  75.8 0.2 select_reduce_fusion.2
  76.0 0.1 collective-permute-start
  76.1 1.2 %collective-permute-done = f32[8,7]{0,1:T(8,128)S(1)} collective-permute-done((f32[8,7]{0,1:T(8,128)S(1)}, f32[8,7]{0,1:T(8,128)S(1)}, u32[]{:S(2)}, u32[]{:S(2)}) %collective-permute-start) | collective-permute-done | bytes 256 | tf_op jit(solution)/shard_map/while/body/eval_jaxpr/ppermute | solution.py:56
  77.2 0.0 collective-permute-start.1
  77.2 3.6 %collective-permute-done.1 = f32[8,7]{0,1:T(8,128)S(1)} collective-permute-done((f32[8,7]{0,1:T(8,128)S(1)}, f32[8,7]{0,1:T(8,128)S(1)}, u32[]{:S(2)}, u32[]{:S(2)}) %collective-permute-start.1) | collective-permute-done | bytes 256 | tf_op jit(solution)/shard_map/while/body/eval_jaxpr/ppermute | solution.py:56
  80.8 1.4 %collective-permute-start.2 = (f32[8,7]{0,1:T(8,128)S(1)}, f32[8,7]{0,1:T(8,128)S(1)}, u32[]{:S(2)}, u32[]{:S(2)}) collective-permute-start(f32[8,7]{0,1:T(8,128)S(1)} %add.81), channel_id=1, source_target_pairs={{0,16},{4,20},{8,24},{12,28},{16,0},{20,4},{24,8},{28,12},{1,17},{... | collective-permute-start | bytes 680 | tf_op jit(solution)/shard_map/while/body/eval_jaxpr/ppermute | solution.py:56
  82.3 2.2 %collective-permute-done.2 = f32[8,7]{0,1:T(8,128)S(1)} collective-permute-done((f32[8,7]{0,1:T(8,128)S(1)}, f32[8,7]{0,1:T(8,128)S(1)}, u32[]{:S(2)}, u32[]{:S(2)}) %collective-permute-start.2) | collective-permute-done | bytes 256 | tf_op jit(solution)/shard_map/while/body/eval_jaxpr/ppermute | solution.py:56
  84.5 0.1 multiply_subtract_fusion.3
  84.6 0.2 select_reduce_fusion.2
  84.8 0.1 collective-permute-start
  84.9 1.2 %collective-permute-done = f32[8,7]{0,1:T(8,128)S(1)} collective-permute-done((f32[8,7]{0,1:T(8,128)S(1)}, f32[8,7]{0,1:T(8,128)S(1)}, u32[]{:S(2)}, u32[]{:S(2)}) %collective-permute-start) | collective-permute-done | bytes 256 | tf_op jit(solution)/shard_map/while/body/eval_jaxpr/ppermute | solution.py:56
  86.0 0.0 collective-permute-start.1
  86.0 3.6 %collective-permute-done.1 = f32[8,7]{0,1:T(8,128)S(1)} collective-permute-done((f32[8,7]{0,1:T(8,128)S(1)}, f32[8,7]{0,1:T(8,128)S(1)}, u32[]{:S(2)}, u32[]{:S(2)}) %collective-permute-start.1) | collective-permute-done | bytes 256 | tf_op jit(solution)/shard_map/while/body/eval_jaxpr/ppermute | solution.py:56
  89.6 1.4 %collective-permute-start.2 = (f32[8,7]{0,1:T(8,128)S(1)}, f32[8,7]{0,1:T(8,128)S(1)}, u32[]{:S(2)}, u32[]{:S(2)}) collective-permute-start(f32[8,7]{0,1:T(8,128)S(1)} %add.81), channel_id=1, source_target_pairs={{0,16},{4,20},{8,24},{12,28},{16,0},{20,4},{24,8},{28,12},{1,17},{... | collective-permute-start | bytes 680 | tf_op jit(solution)/shard_map/while/body/eval_jaxpr/ppermute | solution.py:56
  91.1 2.2 %collective-permute-done.2 = f32[8,7]{0,1:T(8,128)S(1)} collective-permute-done((f32[8,7]{0,1:T(8,128)S(1)}, f32[8,7]{0,1:T(8,128)S(1)}, u32[]{:S(2)}, u32[]{:S(2)}) %collective-permute-start.2) | collective-permute-done | bytes 256 | tf_op jit(solution)/shard_map/while/body/eval_jaxpr/ppermute | solution.py:56
  93.3 0.5 multiply_subtract_fusion.1
  (26 shorter events, 0.2 us)
Async XLA Ops:
  7.2 15.8 %copy-start = (s32[1,8192]{1,0:T(1,128)S(1)}, s32[1,8192]{1,0:T(1,128)}, u32[]{:S(2)}) copy-start(s32[1,8192]{1,0:T(1,128)} %param.13) | copy-start | bytes 98308
  7.2 15.8 %copy-start.1 = (bf16[1,8192]{1,0:T(2,128)(2,1)S(1)}, bf16[1,8192]{1,0:T(2,128)(2,1)}, u32[]{:S(2)}) copy-start(bf16[1,8192]{1,0:T(2,128)(2,1)} %param.14) | copy-start | bytes 49156
  7.2 34.3 %copy-start.3 = (f32[8]{0:T(128)S(1)}, f32[8]{0:T(128)}, u32[]{:S(2)}) copy-start(f32[8]{0:T(128)} %param.17) | copy-start | bytes 100
  7.2 34.3 %copy-start.2 = (f32[8]{0:T(128)S(1)}, f32[8]{0:T(128)}, u32[]{:S(2)}) copy-start(f32[8]{0:T(128)} %param.18) | copy-start | bytes 100
  7.2 59.7 %copy-start.4 = (f32[8]{0:T(128)S(1)}, f32[8]{0:T(128)}, u32[]{:S(2)}) copy-start(f32[8]{0:T(128)} %param.19) | copy-start | bytes 100
  7.2 34.3 %reduce-scatter.2.cloned.1.call-start = ((), (), s32[]{:S(2)}) async-start(), calls=%async_computation.2 | async-start | bytes 163840 | tf_op jit(solution)/shard_map/reduce_scatter | solution.py:33
  24.9 8.0 %all-to-all-start = ((bf16[8,2,512]{2,1,0:T(2,128)(2,1)}), bf16[8,2,512]{2,1,0:T(2,128)(2,1)S(1)}, u32[]{:S(2)}, u32[]{:S(2)}) async-start(bf16[8,2,512]{2,1,0:T(2,128)(2,1)} %reshape.89), calls=%async_computation | async-start | bytes 32768 | tf_op jit(solution)/shard_map/all_to_all | solution.py:27
  67.2 1.2 %collective-permute-start = (f32[8,7]{0,1:T(8,128)S(1)}, f32[8,7]{0,1:T(8,128)S(1)}, u32[]{:S(2)}, u32[]{:S(2)}) collective-permute-start(f32[8,7]{0,1:T(8,128)S(1)} %select_reduce_fusion.2), channel_id=1, source_target_pairs={{0,4},{4,0},{8,12},{12,8},{16,20},{20,16},{24,28},{28,24},{1,5},{5... | collective-permute-start | bytes 680 | tf_op jit(solution)/shard_map/while/body/eval_jaxpr/ppermute | solution.py:56
  68.5 3.6 %collective-permute-start.1 = (f32[8,7]{0,1:T(8,128)S(1)}, f32[8,7]{0,1:T(8,128)S(1)}, u32[]{:S(2)}, u32[]{:S(2)}) collective-permute-start(f32[8,7]{0,1:T(8,128)S(1)} %add.80), channel_id=1, source_target_pairs={{0,8},{4,12},{8,0},{12,4},{16,24},{20,28},{24,16},{28,20},{1,9},{5... | collective-permute-start | bytes 680 | tf_op jit(solution)/shard_map/while/body/eval_jaxpr/ppermute | solution.py:56
  72.1 3.6 %collective-permute-start.2 = (f32[8,7]{0,1:T(8,128)S(1)}, f32[8,7]{0,1:T(8,128)S(1)}, u32[]{:S(2)}, u32[]{:S(2)}) collective-permute-start(f32[8,7]{0,1:T(8,128)S(1)} %add.81), channel_id=1, source_target_pairs={{0,16},{4,20},{8,24},{12,28},{16,0},{20,4},{24,8},{28,12},{1,17},{... | collective-permute-start | bytes 680 | tf_op jit(solution)/shard_map/while/body/eval_jaxpr/ppermute | solution.py:56
  76.0 1.2 %collective-permute-start = (f32[8,7]{0,1:T(8,128)S(1)}, f32[8,7]{0,1:T(8,128)S(1)}, u32[]{:S(2)}, u32[]{:S(2)}) collective-permute-start(f32[8,7]{0,1:T(8,128)S(1)} %select_reduce_fusion.2), channel_id=1, source_target_pairs={{0,4},{4,0},{8,12},{12,8},{16,20},{20,16},{24,28},{28,24},{1,5},{5... | collective-permute-start | bytes 680 | tf_op jit(solution)/shard_map/while/body/eval_jaxpr/ppermute | solution.py:56
  77.2 3.6 %collective-permute-start.1 = (f32[8,7]{0,1:T(8,128)S(1)}, f32[8,7]{0,1:T(8,128)S(1)}, u32[]{:S(2)}, u32[]{:S(2)}) collective-permute-start(f32[8,7]{0,1:T(8,128)S(1)} %add.80), channel_id=1, source_target_pairs={{0,8},{4,12},{8,0},{12,4},{16,24},{20,28},{24,16},{28,20},{1,9},{5... | collective-permute-start | bytes 680 | tf_op jit(solution)/shard_map/while/body/eval_jaxpr/ppermute | solution.py:56
  80.8 3.6 %collective-permute-start.2 = (f32[8,7]{0,1:T(8,128)S(1)}, f32[8,7]{0,1:T(8,128)S(1)}, u32[]{:S(2)}, u32[]{:S(2)}) collective-permute-start(f32[8,7]{0,1:T(8,128)S(1)} %add.81), channel_id=1, source_target_pairs={{0,16},{4,20},{8,24},{12,28},{16,0},{20,4},{24,8},{28,12},{1,17},{... | collective-permute-start | bytes 680 | tf_op jit(solution)/shard_map/while/body/eval_jaxpr/ppermute | solution.py:56
  84.8 1.2 %collective-permute-start = (f32[8,7]{0,1:T(8,128)S(1)}, f32[8,7]{0,1:T(8,128)S(1)}, u32[]{:S(2)}, u32[]{:S(2)}) collective-permute-start(f32[8,7]{0,1:T(8,128)S(1)} %select_reduce_fusion.2), channel_id=1, source_target_pairs={{0,4},{4,0},{8,12},{12,8},{16,20},{20,16},{24,28},{28,24},{1,5},{5... | collective-permute-start | bytes 680 | tf_op jit(solution)/shard_map/while/body/eval_jaxpr/ppermute | solution.py:56
  86.0 3.6 %collective-permute-start.1 = (f32[8,7]{0,1:T(8,128)S(1)}, f32[8,7]{0,1:T(8,128)S(1)}, u32[]{:S(2)}, u32[]{:S(2)}) collective-permute-start(f32[8,7]{0,1:T(8,128)S(1)} %add.80), channel_id=1, source_target_pairs={{0,8},{4,12},{8,0},{12,4},{16,24},{20,28},{24,16},{28,20},{1,9},{5... | collective-permute-start | bytes 680 | tf_op jit(solution)/shard_map/while/body/eval_jaxpr/ppermute | solution.py:56
  89.6 3.6 %collective-permute-start.2 = (f32[8,7]{0,1:T(8,128)S(1)}, f32[8,7]{0,1:T(8,128)S(1)}, u32[]{:S(2)}, u32[]{:S(2)}) collective-permute-start(f32[8,7]{0,1:T(8,128)S(1)} %add.81), channel_id=1, source_target_pairs={{0,16},{4,20},{8,24},{12,28},{16,0},{20,4},{24,8},{28,12},{1,17},{... | collective-permute-start | bytes 680 | tf_op jit(solution)/shard_map/while/body/eval_jaxpr/ppermute | solution.py:56
Sparse Core Ops, SparseCore 0:
  21.8 19.6 reduce-scatter.1
